TPU v7x, 256 devices: a whole 4x4x8 slice. The times are simulated.
256 devices in a mesh: expert: 64 (over x, z, core), rep: 4 (over y).
Axes of the slice: x: 4, y: 4, z: 8, core: 2. Of those that a mesh axis runs over, the one named last changes fastest.
Arguments:
- features: bfloat16 [32768, 1024], P(('expert', 'rep')), may hold values from -20 to 20
- readout: bfloat16 [32768, 1024], P(('expert', 'rep')), may hold values from -20 to 20
- up_weight: bfloat16 [64, 1024, 2048], P('expert'), may hold values from -0.1875 to 0.1875
- down_weight: bfloat16 [64, 2048, 1024], P('expert'), may hold values from -0.125 to 0.125
- expert_ids: int32 [32768, 2], P(('expert', 'rep')), may hold values from 0 to 63, all different within a row; in each aligned block of 128 rows (0 to 127, 128 to 255, ...) at most 5 rows name the same one
- gate_values: float32 [32768, 2], P(('expert', 'rep')), may hold values from 0.2 to 1
Outputs:
- grad_up: bfloat16 [64, 1024, 2048], P('expert', 'rep')
- input_grad: float32 [32768, 1024], P(('expert', 'rep'))
- penalty: float32 [], replicated
Inputs may be any that keep to these rules, and one draw needn't show every extreme that they name: `expert_ids`: each row names 2 different experts. In each aligned block of 128 rows (the rows of one device) no expert is named more than 5 times, a bound that some block reaches.
All inputs are finite; a program needn't handle non-finite values.
Results may differ from a plain program's by a relative error of at most 0.01.
Values may be sent and summed in bfloat16 or wider, within the bound.
A program may use at most 128 MiB of HBM per device.

v0:
```python
import functools

import jax
import jax.numpy as jnp
from jax import lax
from jax.sharding import Mesh
from jax.sharding import PartitionSpec as P

EXPERT = ("expert_0", "expert_1", "expert_2")
EXPERT_REP = ("expert_0", "expert_1", "expert_2", "rep")


def grouped_exchange(shard, axis, split_dim, concat_dim, work, item_dim, out_dim):
    items = jax.tree.leaves(shard)[0].shape[item_dim]
    count = 2 if items % 2 == 0 else 1
    done = []
    for k in range(count):
        group = jax.tree.map(
            lambda a: lax.slice_in_dim(
                a, k * (items // count), (k + 1) * (items // count), axis=item_dim
            ),
            shard,
        )
        done.append(
            work(
                lax.all_to_all(
                    group, axis, split_axis=split_dim, concat_axis=concat_dim, tiled=True
                )
            )
        )
    return jax.tree.map(lambda *parts: jnp.concatenate(parts, axis=out_dim), *done)


def in_blocks(shard, dim, count):
    before, after = (shard.shape[:dim], shard.shape[dim + 1 :])
    return jnp.moveaxis(shard.reshape(*before, count, -1, *after), dim, 0)


def in_order(tiles, dim):
    tiles = jnp.moveaxis(tiles, 0, dim)
    dims = tiles.shape
    return tiles.reshape(*dims[:dim], dims[dim] * dims[dim + 1], *dims[dim + 2 :])


def exchange_in_order(tiles, axes, turns):
    dims = [lax.axis_size(a) for a in axes]
    tiles = tiles.reshape(*dims, *tiles.shape[1:])
    for k in turns:
        tiles = lax.all_to_all(tiles, axes[k], split_axis=k, concat_axis=k, tiled=True)
    return tiles.reshape(-1, *tiles.shape[len(axes) :])


def exchange_by_chip(shard, groups, turns, split_dim, concat_dim):
    count = lax.axis_size(groups[0]) * lax.axis_size(groups[1])
    tiles = in_blocks(shard, split_dim, count)
    return in_order(exchange_in_order(tiles, groups, turns), concat_dim)


def by_axis(shard, axes):
    return functools.reduce(lax.psum, axes, shard)


def silu_slopes(pre_act):
    logistic = jax.nn.sigmoid(pre_act)
    first = logistic * (1.0 + pre_act * (1.0 - logistic))
    second = logistic * (1.0 - logistic) * (2.0 + pre_act * (1.0 - 2.0 * logistic))
    return (first, second)


def contract_last(left, right):
    return lax.dot_general(
        left, right, (((1,), (1,)), ((), ())), preferred_element_type=jnp.float32
    )


def contract_first(left, right):
    return lax.dot_general(
        left, right, (((0,), (0,)), ((), ())), preferred_element_type=jnp.float32
    )


def expert_hidden(slot_x, slot_r, up_matrix, down_matrix):
    pre_act = jnp.dot(slot_x, up_matrix, preferred_element_type=jnp.float32)
    projected = contract_last(slot_r, down_matrix)
    first, second = silu_slopes(pre_act)
    scaled = (first * projected).astype(jnp.bfloat16)
    return (scaled, pre_act, projected)


def body(features, readout, up_weight, down_weight, expert_ids, gate_values):
    tok_rows, width = features.shape
    hidden_units = up_weight.shape[2]
    groups = lax.axis_size(EXPERT)
    copies = lax.axis_size("rep")
    expert_total = groups * up_weight.shape[0]
    capacity = (9 * tok_rows * 2 + 8 * expert_total - 1) // (8 * expert_total)
    up_matrix = up_weight[0]
    down_matrix = down_weight[0]
    flat_ids = expert_ids.reshape(-1)
    onehot = (flat_ids[:, None] == jnp.arange(expert_total, dtype=jnp.int32)[None, :]).astype(
        jnp.int32
    )
    earlier = jnp.cumsum(onehot, axis=0) - onehot
    slot_index = jnp.sum(earlier * onehot, axis=1)
    position = flat_ids * capacity + slot_index
    placing = (
        jnp.arange(expert_total * capacity, dtype=jnp.int32)[:, None] == position[None, :]
    ).astype(jnp.bfloat16)
    paired = jnp.repeat(jnp.concatenate([features, readout], axis=1), 2, axis=0)
    packed = jnp.dot(placing, paired, preferred_element_type=jnp.float32).astype(jnp.bfloat16)
    packed = packed.reshape(expert_total, capacity, 2 * width)
    send_x = packed[:, :, :width]
    send_r = packed[:, :, width:]

    def expert_slots(received):
        recv_x, recv_r = received
        sources, items = (recv_x.shape[0], recv_x.shape[1])
        flat_x = recv_x.reshape(sources * items, width)
        flat_r = recv_r.reshape(sources * items, width)
        scaled, pre_act, projected = expert_hidden(flat_x, flat_r, up_matrix, down_matrix)
        output = contract_last(scaled, up_matrix).astype(jnp.bfloat16)
        return (
            output.reshape(sources, items, width),
            scaled.reshape(sources, items, hidden_units),
            pre_act.reshape(sources, items, hidden_units),
            projected.reshape(sources, items, hidden_units),
            recv_x,
            recv_r,
        )

    results = grouped_exchange((send_x, send_r), EXPERT, 0, 0, expert_slots, 1, 1)
    expert_out, kept_scaled, kept_pre, kept_proj, kept_x, kept_r = results
    returned = exchange_by_chip(expert_out, (("expert_0", "expert_1"), "expert_2"), (1, 0), 0, 0)
    pair_out = contract_first(placing, returned.reshape(expert_total * capacity, width)).reshape(
        tok_rows, 2, width
    )
    input_grad = (
        readout.astype(jnp.float32)
        + gate_values[:, 0:1] * pair_out[:, 0]
        + gate_values[:, 1:2] * pair_out[:, 1]
    )
    squares = by_axis(jnp.sum(input_grad * input_grad), EXPERT_REP)
    penalty = squares / (2.0 * tok_rows * groups * copies * width)
    cotangent = (
        (gate_values[:, :, None] * input_grad[:, None, :])
        .reshape(2 * tok_rows, width)
        .astype(jnp.bfloat16)
    )
    send_w = jnp.dot(placing, cotangent, preferred_element_type=jnp.float32).astype(jnp.bfloat16)
    send_w = send_w.reshape(expert_total, capacity, width)
    recv_w = exchange_by_chip(send_w, (("expert_0", "expert_1"), "expert_2"), (1, 0), 0, 0)
    slots_total = recv_w.shape[0] * recv_w.shape[1]
    flat_w = recv_w.reshape(slots_total, width)
    flat_x = kept_x.reshape(slots_total, width)
    scaled = kept_scaled.reshape(slots_total, hidden_units)
    pre_act = kept_pre.reshape(slots_total, hidden_units)
    projected = kept_proj.reshape(slots_total, hidden_units)
    first, second = silu_slopes(pre_act)
    slope_grad = jnp.dot(flat_w, up_matrix, preferred_element_type=jnp.float32)
    pre_grad = (slope_grad * projected * second).astype(jnp.bfloat16)
    summed = lax.psum_scatter(
        (contract_first(flat_w, scaled) + contract_first(flat_x, pre_grad)).astype(jnp.bfloat16),
        "rep",
        scatter_dimension=0,
        tiled=True,
    )
    grad_up = summed[None]
    return (grad_up, input_grad, penalty)


def solution(mesh):
    finer = Mesh(
        mesh.devices.reshape(4, 8, 2, mesh.shape["rep"]),
        ("expert_0", "expert_1", "expert_2", "rep"),
    )
    return jax.shard_map(
        body,
        mesh=finer,
        in_specs=(
            P(EXPERT_REP, None),
            P(EXPERT_REP, None),
            P(EXPERT, None, None),
            P(EXPERT, None, None),
            P(EXPERT_REP, None),
            P(EXPERT_REP, None),
        ),
        out_specs=(P(EXPERT, "rep", None), P(EXPERT_REP, None), P()),
        check_vma=False,
    )
```

profile of v0, /device:TPU:1, one launch (start us, length us, event | category | flops | bytes accessed | tf_op | source)
XLA Modules:
  0.0 238.7 jit_solution(11725500386783902744)
XLA Ops:
  7.2 0.8 copy.14
  9.2 1.1 pad_maximum_fusion
  12.4 1.1 fusion.43
  13.6 41.3 %all_to_all.30 = bf16[64,5,1024]{2,1,0:T(8,128)(2,1)S(1)} all-to-all(bf16[64,5,1024]{2,1,0:T(8,128)(2,1)S(1)} %get-tuple-element.5), channel_id=1, replica_groups=mesh['expert_0'=4,'expert_1'=8,'expert_2'=2,'rep'=4] {'expert_0','expert..., dimensions={0} | all-to-all | bytes 1310720 | tf_op jit(solution)/shard_map/all_to_all | solution.py:26
  54.9 6.2 %all-to-all-start.1 = ((bf16[64,5,1024]{2,1,0:T(8,128)(2,1)}), bf16[64,5,1024]{2,1,0:T(8,128)(2,1)S(1)}, u32[]{:S(2)}, u32[]{:S(2)}) async-start(bf16[64,5,1024]{2,1,0:T(8,128)(2,1)} %get-tuple-element.6), calls=%async_computation.1 | async-start | bytes 2097152 | tf_op jit(solution)/shard_map/all_to_all | solution.py:26
  61.4 5.5 %fusion.6 = f32[320,2048]{1,0:T(8,128)} fusion(bf16[320,1024]{1,0:T(8,128)(2,1)S(1)} %reshape.83, bf16[1,1024,2048]{2,1,0:T(8,128)(2,1)} %param.8), kind=kOutput, calls=%fused_computation.7 | convolution fusion | flops 1342177280 | bytes 7471104 | tf_op jit(solution)/shard_map/dot_general | solution.py:83
  66.8 22.8 %all-to-all-done.1 = bf16[64,5,1024]{2,1,0:T(8,128)(2,1)S(1)} async-done(((bf16[64,5,1024]{2,1,0:T(8,128)(2,1)}), bf16[64,5,1024]{2,1,0:T(8,128)(2,1)S(1)}, u32[]{:S(2)}, u32[]{:S(2)}) %all-to-all-start.1) | async-done | bytes 655392 | tf_op jit(solution)/shard_map/all_to_all | solution.py:26
  89.9 6.4 %fusion.20 = (bf16[320,2048]{1,0:T(8,128)(2,1)S(1)}, f32[320,2048]{1,0:T(8,128)}) fusion(f32[320,2048]{1,0:T(8,128)} %fusion.6, bf16[320,1024]{1,0:T(8,128)(2,1)S(1)} %reshape.84, bf16[1,2048,1024]{2,1,0:T(8,128)(2,1)} %param.9), kind=kOutput, calls=%fused_computation.18 | convolution fusion | flops 1348075520 | bytes 11403264 | tf_op jit(solution)/shard_map/dot_general | solution.py:71
  96.3 1.1 copy-done.1
  97.3 1.5 fusion.22
  99.6 4.0 %all_to_all.31 = bf16[32,2,1,5,1024]{4,0,3,2,1:T(8,128)(2,1)S(1)} all-to-all(bf16[32,2,1,5,1024]{4,0,3,2,1:T(8,128)(2,1)S(1)} %copy.18), channel_id=1, replica_groups=mesh['expert_0'=4,'expert_1'=8,'expert_2'=2,'rep'=4] {'expert_2'}, dimensions={1} | all-to-all | bytes 1310720 | tf_op jit(solution)/shard_map/all_to_all | solution.py:49
  103.6 1.5 copy.19
  105.1 5.7 %all-to-all-start.3 = ((bf16[32,2,1,5,1024]{4,1,3,2,0:T(2,128)(2,1)}), bf16[32,2,1,5,1024]{4,1,3,2,0:T(2,128)(2,1)S(1)}, u32[]{:S(2)}, u32[]{:S(2)}) async-start(bf16[32,2,1,5,1024]{4,1,3,2,0:T(2,128)(2,1)} %copy.19), calls=%async_computation.3 | async-start | bytes 1310720 | tf_op jit(solution)/shard_map/all_to_all | solution.py:49
  111.6 16.1 %all-to-all-done.3 = bf16[32,2,1,5,1024]{4,1,3,2,0:T(2,128)(2,1)S(1)} async-done(((bf16[32,2,1,5,1024]{4,1,3,2,0:T(2,128)(2,1)}), bf16[32,2,1,5,1024]{4,1,3,2,0:T(2,128)(2,1)S(1)}, u32[]{:S(2)}, u32[]{:S(2)}) %all-to-all-start.3) | async-done | bytes 655392 | tf_op jit(solution)/shard_map/all_to_all | solution.py:49
  128.6 0.9 multiply_reduce_fusion
  131.7 7.6 %all_to_all.32 = bf16[32,2,1,5,1024]{4,0,3,2,1:T(8,128)(2,1)S(1)} all-to-all(bf16[32,2,1,5,1024]{4,0,3,2,1:T(8,128)(2,1)S(1)} %copy.22), channel_id=1, replica_groups=mesh['expert_0'=4,'expert_1'=8,'expert_2'=2,'rep'=4] {'expert_2'}, dimensions={1} | all-to-all | bytes 1310720 | tf_op jit(solution)/shard_map/all_to_all | solution.py:49
  140.0 22.2 %all_to_all.33 = bf16[32,2,1,5,1024]{4,1,3,2,0:T(2,128)(2,1)S(1)} all-to-all(bf16[32,2,1,5,1024]{4,1,3,2,0:T(2,128)(2,1)S(1)} %copy.23), channel_id=1, replica_groups=mesh['expert_0'=4,'expert_1'=8,'expert_2'=2,'rep'=4] {'expert_0','expert..., dimensions={0} | all-to-all | bytes 1310720 | tf_op jit(solution)/shard_map/all_to_all | solution.py:49
  162.7 5.6 %fusion.44 = f32[1024,2048]{1,0:T(8,128)} fusion(bf16[320,1024]{1,0:T(8,128)(2,1)S(1)} %reshape_reshape_reshape.15, bf16[320,2048]{1,0:T(8,128)(2,1)S(1)} %copy-done.2), kind=kOutput, calls=%fused_computation.54 | convolution fusion | flops 1342177280 | bytes 10354688 | tf_op jit(solution)/shard_map/dot_general | solution.py:77
  168.4 12.3 %add_convert_fusion = bf16[1024,2048]{1,0:T(8,128)(2,1)} fusion(f32[1024,2048]{1,0:T(8,128)} %fusion.44, bf16[320,1024]{1,0:T(8,128)(2,1)S(1)} %copy-done.5, f32[320,2048]{1,0:T(8,128)} %get-tuple-element.10, bf16[320,1024]{1,0:T(8,128)(2,1)S(1)} %reshape_reshape_reshape.15, bf16[1,1024,2048]{2,1,0:T(8,128)(2,1)} %param.8, f32[320,2048]{1,0:T(8,128)} %fusion.6), kind=kOutput, calls=%fused_computation | convolution fusion | flops 2697068544 | bytes 23330816 | tf_op jit(solution)/shard_map/dot_general | solution.py:77
  180.7 8.3 %psum.28 = f32[]{:T(128)} all-reduce(f32[]{:T(128)} %get-tuple-element.3), channel_id=1, replica_groups=mesh['expert_0'=4,'expert_1'=8,'expert_2'=2,'rep'=4] {'expert_0'}, use_global_device_ids=true, to_apply=%region_5.6 | all-reduce | flops 1 | bytes 8 | tf_op jit(solution)/shard_map/psum | solution.py:60
  189.0 15.5 %psum.29 = f32[]{:T(128)} all-reduce(f32[]{:T(128)} %psum.28), channel_id=1, replica_groups=mesh['expert_0'=4,'expert_1'=8,'expert_2'=2,'rep'=4] {'expert_1'}, use_global_device_ids=true, to_apply=%region_6.7 | all-reduce | flops 1 | bytes 8 | tf_op jit(solution)/shard_map/psum | solution.py:60
  204.6 9.3 %psum.30 = f32[]{:T(128)} all-reduce(f32[]{:T(128)} %psum.29), channel_id=1, replica_groups=mesh['expert_0'=4,'expert_1'=8,'expert_2'=2,'rep'=4] {'expert_2'}, use_global_device_ids=true, to_apply=%region_7.8 | all-reduce | flops 1 | bytes 8 | tf_op jit(solution)/shard_map/psum | solution.py:60
  213.8 10.5 %psum.31 = f32[]{:T(128)} all-reduce(f32[]{:T(128)} %psum.30), channel_id=1, replica_groups=mesh['expert_0'=4,'expert_1'=8,'expert_2'=2,'rep'=4] {'rep'}, use_global_device_ids=true, to_apply=%region_8.9 | all-reduce | flops 1 | bytes 8 | tf_op jit(solution)/shard_map/psum | solution.py:60
  225.0 5.7 %reduce-scatter.2.cloned.1.call-done = bf16[256,2048]{1,0:T(8,128)(2,1)} async-done(((bf16[1024,2048]{1,0:T(8,128)(2,1)}), bf16[256,2048]{1,0:T(8,128)(2,1)}) %reduce-scatter.2.cloned.1.call-update) | async-done | bytes 1048592 | tf_op jit(solution)/shard_map/reduce_scatter | solution.py:161
  (50 shorter events, 9.7 us)
Async XLA Ops:
  54.9 34.7 %all-to-all-start.1 = ((bf16[64,5,1024]{2,1,0:T(8,128)(2,1)}), bf16[64,5,1024]{2,1,0:T(8,128)(2,1)S(1)}, u32[]{:S(2)}, u32[]{:S(2)}) async-start(bf16[64,5,1024]{2,1,0:T(8,128)(2,1)} %get-tuple-element.6), calls=%async_computation.1 | async-start | bytes 2097152 | tf_op jit(solution)/shard_map/all_to_all | solution.py:26
  61.4 5.5 %copy-start.4 = (bf16[320,1024]{1,0:T(8,128)(2,1)}, bf16[320,1024]{1,0:T(8,128)(2,1)S(1)}, u32[]{:S(2)}) copy-start(bf16[320,1024]{1,0:T(8,128)(2,1)S(1)} %reshape.83) | copy-start | bytes 1966084
  89.9 7.5 %copy-start.7 = (bf16[1,1024,2048]{2,1,0:T(8,128)(2,1)S(1)}, bf16[1,1024,2048]{2,1,0:T(8,128)(2,1)}, u32[]{:S(2)}) copy-start(bf16[1,1024,2048]{2,1,0:T(8,128)(2,1)} %param.8) | copy-start | bytes 12582916
  96.3 1.1 copy-start.1
  99.2 11.8 %copy-start.6 = (f32[128,2]{0,1:T(2,128)S(1)}, f32[128,2]{0,1:T(2,128)}, u32[]{:S(2)}) copy-start(f32[128,2]{0,1:T(2,128)} %param.11) | copy-start | bytes 3076
  105.1 22.6 %all-to-all-start.3 = ((bf16[32,2,1,5,1024]{4,1,3,2,0:T(2,128)(2,1)}), bf16[32,2,1,5,1024]{4,1,3,2,0:T(2,128)(2,1)S(1)}, u32[]{:S(2)}, u32[]{:S(2)}) async-start(bf16[32,2,1,5,1024]{4,1,3,2,0:T(2,128)(2,1)} %copy.19), calls=%async_computation.3 | async-start | bytes 1310720 | tf_op jit(solution)/shard_map/all_to_all | solution.py:49
  110.8 119.9 %reduce-scatter.2.cloned.1.call-start = ((), (), s32[]{:S(2)}) async-start(), calls=%async_computation.7 | async-start | bytes 5242880 | tf_op jit(solution)/shard_map/reduce_scatter | solution.py:161
  111.5 17.1 %copy-start.3 = (bf16[128,1024]{1,0:T(8,128)(2,1)S(1)}, bf16[128,1024]{1,0:T(8,128)(2,1)}, u32[]{:S(2)}) copy-start(bf16[128,1024]{1,0:T(8,128)(2,1)} %param.7) | copy-start | bytes 786436
  129.5 1.5 copy-start
  140.0 22.7 %copy-start.2 = (bf16[320,2048]{1,0:T(8,128)(2,1)S(1)}, bf16[320,2048]{1,0:T(8,128)(2,1)}, u32[]{:S(2)}) copy-start(bf16[320,2048]{1,0:T(8,128)(2,1)} %copy-done.1) | copy-start | bytes 3932164
  162.7 5.6 %copy-start.5 = (bf16[320,1024]{1,0:T(8,128)(2,1)S(1)}, bf16[320,1024]{1,0:T(8,128)(2,1)}, u32[]{:S(2)}) copy-start(bf16[320,1024]{1,0:T(8,128)(2,1)} %copy-done.4) | copy-start | bytes 1966084
Sparse Core Ops, SparseCore 0:
  180.8 49.8 reduce-scatter.1
where the time goes:
time: 239 us
  blocking collectives  119 us (50%)
  waiting for transfers between devices  44.5 us (19%)
  matrix products  32.7 us (14%)
  between operations  16.1 us (7%)
  starting transfers between devices  12.1 us (5%)
  local copies, waits for them, and re-layouts  11.7 us (5%)
  other arithmetic  2.84 us (1%)
    psum x4, blocking collectives, by_axis(): return functools.reduce(lax.psum, axes, shard)  43.7 us
    all_to_all x1, blocking collectives, grouped_exchange(): lax.all_to_all(group, axis, split_axis=split_dim, concat_axis=concat_dim,...  41.3 us
    all_to_all x3, blocking collectives, exchange_in_order(): lax.all_to_all(tiles, axes[k], split_axis=k, concat_axis=k, tiled=True)  33.7 us
    all_to_all x1, waiting for transfers between devices, grouped_exchange(): lax.all_to_all(group, axis, split_axis=split_dim, concat_axis=concat_dim,...  22.8 us
    dot_general x3, matrix products, contract_first(): lax.dot_general(left, right, (((0,), (0,)), ((), ())), preferred_element_...  18.4 us
    all_to_all x1, waiting for transfers between devices, exchange_in_order(): lax.all_to_all(tiles, axes[k], split_axis=k, concat_axis=k, tiled=True)  16.1 us
    dot_general x2, matrix products, contract_last(): lax.dot_general(left, right, (((1,), (1,)), ((), ())), preferred_element_...  7.93 us
    all_to_all x1, starting transfers between devices, grouped_exchange(): lax.all_to_all(group, axis, split_axis=split_dim, concat_axis=concat_dim,...  6.2 us
  transfers between devices with their start and end apart: 3, of which 3 were waited for; matrix products, arithmetic and copies ran while one was open for 3% of the time, Pallas kernels for 0%

commit v1 on v0

v1 whole, which is shorter than its diff:
```python
import functools

import jax
import jax.numpy as jnp
import numpy as np
from jax import lax
from jax.experimental import pallas as pl
from jax.experimental.pallas import tpu as pltpu
from jax.sharding import PartitionSpec as P

MESH = pl.DeviceIdType.MESH
F32 = jnp.float32
BF16 = jnp.bfloat16
NX, NZ, NC, CAP = 4, 8, 2, 5


def dot(a, b):
    return lax.dot_general(a, b, (((1,), (0,)), ((), ())), preferred_element_type=F32)


def dot_t(a, b):
    return lax.dot_general(a, b, (((1,), (1,)), ((), ())), preferred_element_type=F32)


def kernel(
    dims,
    x_ref, r_ref, up_hbm, down_hbm, ids_ref, gate_ref, pf_ref, pb_ref,
    grad_ref, ig_ref, pen_ref,
    up, down, sz, rz, sx, rx, ax, ar, slope, curve, proj, sg, scaled, pgrad, xt, wt,
    sel, selt, rs_s, rs_r, q_r, q_g, q_y,
    wsem, zs, zr, xs, xr, rss, rsr, qs, qr,
):
    nx, nz, nc, ny, cap = dims
    ng = nx * nc
    tok, width = x_ref.shape
    ff = up.shape[1]
    half = width // 2
    zrow, grow = ng * cap, nz * cap
    slots = nz * zrow
    e = lax.axis_index("expert")
    y = lax.axis_index("rep")
    x = e // (nz * nc)
    z = (e // nc) % nz
    c = e % nc
    g = x * nc + c

    def z_peer(k):
        zt = lax.rem(z + k, nz)
        return zt, ((x * nz + zt) * nc + c, y)

    def g_peer(k):
        gt = lax.rem(g + k, ng)
        return gt, (((gt // nc) * nz + z) * nc + gt % nc, y)

    def y_peer(k):
        yt = lax.rem(y + k, ny)
        return yt, (e, yt)

    load_up = pltpu.make_async_copy(up_hbm.at[0], up, wsem.at[0])
    load_down = pltpu.make_async_copy(down_hbm.at[0], down, wsem.at[1])
    load_up.start()
    load_down.start()

    barrier = pltpu.get_barrier_semaphore()
    peers = (
        [z_peer(k)[1] for k in range(1, nz)]
        + [g_peer(k)[1] for k in range(1, ng)]
        + [y_peer(k)[1] for k in range(1, ny)]
    )
    for peer in peers:
        pl.semaphore_signal(barrier, inc=1, device_id=peer, device_id_type=MESH)

    zorder = sorted(range(1, nz), key=lambda k: (-min(k, nz - k), k))
    gorder = sorted(range(1, ng), key=lambda k: (-min(k, ng - k), k))

    def z_send(st):
        for k in zorder:
            zt, dev = z_peer(k)
            pltpu.make_async_remote_copy(
                src_ref=sz.at[st, zt], dst_ref=rz.at[st, z],
                send_sem=zs.at[st], recv_sem=zr.at[st],
                device_id=dev, device_id_type=MESH,
            ).start()

    def g_send(st):
        for k in gorder:
            gt, dev = g_peer(k)
            pltpu.make_async_remote_copy(
                src_ref=sx.at[st, gt], dst_ref=rx.at[st, g],
                send_sem=xs.at[st], recv_sem=xr.at[st],
                device_id=dev, device_id_type=MESH,
            ).start()

    def wait_all(ref, st, count, sem):
        part = ref.at[st, pl.ds(0, count)]
        pltpu.make_async_copy(part, part, sem.at[st]).wait()

    def z_wait(st):
        wait_all(rz, st, nz - 1, zr)
        rz[st, z] = sz[st, z]

    def g_wait(st):
        wait_all(rx, st, ng - 1, xr)
        rx[st, g] = sx[st, g]

    def flat(ref, st):
        v = ref[st].astype(F32)
        return v.reshape(slots, half).astype(BF16)

    def put(ref, st, v):
        shape = ref.shape[1:]
        ref[st] = v.reshape(shape).astype(BF16)

    n_exp = nz * ng
    col_e = lax.broadcasted_iota(jnp.int32, (tok, n_exp), 1)
    onehots = []
    orders = []
    for k in range(2):
        v = ids_ref[:, k : k + 1]
        rest = v // nc if nc > 1 else v
        q = (rest % nz) * ng + (rest // nz) * nc + (v % nc if nc > 1 else 0)
        orders.append(q)
        onehots.append(jnp.where(col_e == q, 1.0, 0.0).astype(F32))
    count = (onehots[0] + onehots[1]).astype(BF16)
    ti = lax.broadcasted_iota(jnp.int32, (tok, tok), 0)
    tj = lax.broadcasted_iota(jnp.int32, (tok, tok), 1)
    lower = jnp.where(tj < ti, 1.0, 0.0).astype(BF16)
    earlier = dot(lower, count)
    col_s = lax.broadcasted_iota(jnp.int32, (tok, slots), 1).astype(F32)
    for k in range(2):
        slot = jnp.sum(onehots[k] * earlier, axis=1, keepdims=True)
        pos = orders[k].astype(F32) * cap + slot
        m = jnp.where(col_s == pos, 1.0, 0.0).astype(F32)
        sel[k] = m.astype(BF16)
        selt[k] = m.T.astype(BF16)

    both = (selt[0].astype(F32) + selt[1].astype(F32)).astype(BF16)
    for h in range(2):
        put(sz, h, dot(both, x_ref[:, h * half : (h + 1) * half]))
    pl.semaphore_wait(barrier, len(peers))
    z_send(0)
    z_send(1)
    for h in range(2):
        put(sz, 2 + h, dot(both, r_ref[:, h * half : (h + 1) * half]))
        z_send(2 + h)

    def forward(st):
        z_wait(st)
        put(sx, st, dot(pf_ref[...], flat(rz, st)))
        g_send(st)

    tile = 256
    forward(0)
    forward(1)
    load_up.wait()
    load_down.wait()
    for h in range(2):
        g_wait(h)
        ax[:, h * half : (h + 1) * half] = flat(rx, h)

    @pl.loop(0, ff // tile)
    def _(i):
        n = pl.ds(pl.multiple_of(i * tile, tile), tile)
        p = dot(ax[...], up[:, n])
        s = 1.0 / (1.0 + jnp.exp(-p))
        slope[:, n] = s * (1.0 + p * (1.0 - s))
        curve[:, n] = s * (1.0 - s) * (2.0 + p * (1.0 - 2.0 * s))

    forward(2)
    forward(3)
    g_wait(2)
    ar[:, :half] = flat(rx, 2)

    @pl.loop(0, ff // tile)
    def _(i):
        n = pl.ds(pl.multiple_of(i * tile, tile), tile)
        proj[:, n] = dot_t(ar[:, :half], down[n, :half])

    g_wait(3)
    ar[:, half:] = flat(rx, 3)

    @pl.loop(0, ff // tile)
    def _(i):
        n = pl.ds(pl.multiple_of(i * tile, tile), tile)
        p = proj[:, n] + dot_t(ar[:, half:], down[n, half:])
        scaled[:, n] = (slope[:, n] * p).astype(BF16)
        proj[:, n] = p * curve[:, n]

    for h in range(2):
        for i in range(half // tile if half > tile else 1):
            w = min(tile, half)
            lo = i * w
            v = dot_t(scaled[...], up[h * half + lo : h * half + lo + w, :])
            sx[4 + h, :, :, lo : lo + w] = v.reshape(ng, grow, w).astype(BF16)
        g_send(4 + h)
    for h in range(2):
        g_wait(4 + h)
        put(sz, 4 + h, dot(pb_ref[...], flat(rx, 4 + h)))
        z_send(4 + h)

    xt[...] = ax[...].astype(F32).T.astype(BF16)

    squares = jnp.zeros((8, 128), F32)
    for h in range(2):
        cols = slice(h * half, (h + 1) * half)
        z_wait(4 + h)
        got = flat(rz, 4 + h)
        g0 = gate_ref[:, 0:1]
        g1 = gate_ref[:, 1:2]
        ig = r_ref[:, cols].astype(F32) + g0 * dot(sel[0], got) + g1 * dot(sel[1], got)
        ig_ref[:, cols] = ig
        cot = dot(selt[0], (g0 * ig).astype(BF16)) + dot(selt[1], (g1 * ig).astype(BF16))
        put(sz, 6 + h, cot)
        z_send(6 + h)
        sq = (ig * ig).reshape(tok // 8, 8, half // 128, 128)
        squares = squares + jnp.sum(jnp.sum(sq, axis=0), axis=1)

    def q_send(buf, me, peer_of, n, st):
        for k in range(1, n):
            _, dev = peer_of(k)
            pltpu.make_async_remote_copy(
                src_ref=buf.at[me], dst_ref=buf.at[me],
                send_sem=qs.at[st], recv_sem=qr.at[st],
                device_id=dev, device_id_type=MESH,
            ).start()

    def q_wait(buf, n, st):
        part = buf.at[pl.ds(0, n - 1)]
        pltpu.make_async_copy(part, part, qr.at[st]).wait()
        pltpu.make_async_copy(part, part, qs.at[st]).wait()
        total = buf[0]
        for i in range(1, n):
            total = total + buf[i]
        return total

    q_r[z] = squares
    q_send(q_r, z, z_peer, nz, 0)

    for st in (6, 7):
        forward(st)
    q_g[g] = q_wait(q_r, nz, 0)
    q_send(q_g, g, g_peer, ng, 1)

    g_wait(6)
    first = flat(rx, 6)
    wt[:half] = first.astype(F32).T.astype(BF16)

    @pl.loop(0, ff // tile)
    def _(i):
        n = pl.ds(pl.multiple_of(i * tile, tile), tile)
        sg[:, n] = dot(flat(rx, 6), up[:half, n])

    g_wait(7)
    wt[half:] = flat(rx, 7).astype(F32).T.astype(BF16)

    @pl.loop(0, ff // tile)
    def _(i):
        n = pl.ds(pl.multiple_of(i * tile, tile), tile)
        s = sg[:, n] + dot(flat(rx, 7), up[half:, n])
        pgrad[:, n] = (s * proj[:, n]).astype(BF16)

    q_y[y] = q_wait(q_g, ng, 1)
    q_send(q_y, y, y_peer, ny, 2)

    rows = width // ny
    parts = rs_s.shape[2]
    piece = ff // 2 // parts

    def unit(block, d, j):
        rb = pl.ds(pl.multiple_of(block * rows, rows), rows)
        cb = pl.ds(pl.multiple_of(d * (ff // 2) + j * piece, piece), piece)
        v = dot(wt[rb, :], scaled[:, cb]) + dot(xt[rb, :], pgrad[:, cb])
        return v.astype(BF16).astype(F32), cb

    def rs_copy(t, d, j):
        _, dev = y_peer(1 if d == 0 else ny - 1)
        return pltpu.make_async_remote_copy(
            src_ref=rs_s.at[d, t, j], dst_ref=rs_r.at[d, t, j],
            send_sem=rss.at[d, t, j], recv_sem=rsr.at[d, t, j],
            device_id=dev, device_id_type=MESH,
        )

    for t in range(ny):
        @pl.loop(0, parts)
        def _(j):
            for d in range(2):
                step = t + 1
                block = lax.rem(y + (ny - step if d == 0 else step), ny)
                v, cb = unit(block, d, j)
                if t > 0:
                    rs_copy(t - 1, d, j).wait_recv()
                    v = v + rs_r[d, t - 1, j].astype(F32)
                if t < ny - 1:
                    rs_s[d, t, j] = v.astype(BF16)
                    rs_copy(t, d, j).start()
                else:
                    grad_ref[0, :, cb] = v.astype(BF16)

    total = q_wait(q_y, ny, 2)
    total = jnp.sum(jnp.sum(total, axis=0, keepdims=True), axis=1, keepdims=True)
    pen_ref[...] = jnp.broadcast_to(total, pen_ref.shape)

    @pl.loop(0, parts)
    def _(j):
        for t in range(ny - 1):
            for d in range(2):
                rs_copy(t, d, j).wait_send()

    for st in range(8):
        wait_all(sz, st, nz - 1, zs)
        wait_all(sx, st, ng - 1, xs)


def regroup(outer, inner, cap):
    n = outer * inner * cap
    src = np.arange(n).reshape(outer, inner, cap).transpose(1, 0, 2).reshape(-1)
    return jnp.asarray(np.eye(n, dtype=np.float32)[src], BF16)


def body(dims, features, readout, up_weight, down_weight, expert_ids, gate_values):
    nx, nz, nc, ny, cap = dims
    ng = nx * nc
    tok, width = features.shape
    ff = up_weight.shape[2]
    half = width // 2
    slots = nz * ng * cap
    parts = max(1, ff // 2 // 256)
    vm = pl.BlockSpec(memory_space=pltpu.VMEM)
    hbm = pl.BlockSpec(memory_space=pl.ANY)
    dma = pltpu.SemaphoreType.DMA
    zbuf = pltpu.VMEM((8, nz, ng * cap, half), BF16)
    gbuf = pltpu.VMEM((8, ng, nz * cap, half), BF16)
    wide = pltpu.VMEM((slots, ff), F32)
    ring = pltpu.VMEM((2, ny - 1, parts, width // ny, ff // 2 // parts), BF16)
    grad, ig, pen = pl.pallas_call(
        functools.partial(kernel, dims),
        out_shape=(
            jax.ShapeDtypeStruct((1, width // ny, ff), BF16),
            jax.ShapeDtypeStruct((tok, width), F32),
            jax.ShapeDtypeStruct((8, 128), F32),
        ),
        in_specs=[vm, vm, hbm, hbm, vm, vm, vm, vm],
        out_specs=(vm, vm, vm),
        scratch_shapes=[
            pltpu.VMEM((width, ff), BF16),
            pltpu.VMEM((ff, width), BF16),
            zbuf, zbuf, gbuf, gbuf,
            pltpu.VMEM((slots, width), BF16),
            pltpu.VMEM((slots, width), BF16),
            wide, wide, wide, wide,
            pltpu.VMEM((slots, ff), BF16),
            pltpu.VMEM((slots, ff), BF16),
            pltpu.VMEM((width, slots), BF16),
            pltpu.VMEM((width, slots), BF16),
            pltpu.VMEM((2, tok, slots), BF16),
            pltpu.VMEM((2, slots, tok), BF16),
            ring, ring,
            pltpu.VMEM((nz, 8, 128), F32),
            pltpu.VMEM((ng, 8, 128), F32),
            pltpu.VMEM((ny, 8, 128), F32),
            dma((2,)), dma((8,)), dma((8,)), dma((8,)), dma((8,)),
            dma((2, ny - 1, parts)), dma((2, ny - 1, parts)),
            dma((3,)), dma((3,)),
        ],
        compiler_params=pltpu.CompilerParams(
            collective_id=0, has_side_effects=True, vmem_limit_bytes=67043328
        ),
    )(
        features, readout, up_weight, down_weight, expert_ids, gate_values,
        regroup(nz, ng, cap), regroup(ng, nz, cap),
    )
    groups = nz * ng
    penalty = pen[0, 0] / (2.0 * tok * groups * ny * width)
    return grad, ig, penalty


def solution(mesh, dims=None):
    if dims is None:
        dims = (NX, NZ, NC, mesh.shape["rep"], CAP)
    both = ("expert", "rep")
    return jax.shard_map(
        functools.partial(body, dims),
        mesh=mesh,
        in_specs=(
            P(both, None), P(both, None),
            P("expert", None, None), P("expert", None, None),
            P(both, None), P(both, None),
        ),
        out_specs=(P("expert", "rep", None), P(both, None), P()),
        check_vma=False,
    )
```

time: 239 us -> 145 us (0.61)
  Pallas kernels: 0 us -> 134 us
  blocking collectives: 119 us -> 0 us
  waiting for transfers between devices: 44.5 us -> 0 us
  matrix products: 32.7 us -> 0 us
  between operations: 16.1 us -> 2.42 us
  starting transfers between devices: 12.1 us -> 0 us
  local copies, waits for them, and re-layouts: 11.7 us -> 8.21 us
  other arithmetic: 2.84 us -> 0 us
    pallas_call x0 -> x1, Pallas kernels: none -> 134 us  [body(): pl.pallas_call(functools.partial(kernel, dims), out_shape=(jax.ShapeDtype...]
    all_to_all x4 -> x0, blocking collectives: 75 us -> none  [the longest x1 41.3 us: grouped_exchange(): lax.all_to_all(group, axis, split_axis=split_dim, concat_axis=concat_dim,...]
    psum x4 -> x0, blocking collectives: 43.7 us -> none  [by_axis(): return functools.reduce(lax.psum, axes, shard)]
    all_to_all x2 -> x0, waiting for transfers between devices: 38.9 us -> none  [the longest x1 22.8 us: grouped_exchange(): lax.all_to_all(group, axis, split_axis=split_dim, concat_axis=concat_dim,...]
    dot_general x8 -> x0, matrix products: 32.7 us -> none  [the longest x3 18.4 us: contract_first(): lax.dot_general(left, right, (((0,), (0,)), ((), ())), preferred_element_...]
    all_to_all x2 -> x0, starting transfers between devices: 11.9 us -> none  [the longest x1 6.2 us: grouped_exchange(): lax.all_to_all(group, axis, split_axis=split_dim, concat_axis=concat_dim,...]
    reduce_scatter x1 -> x0, waiting for transfers between devices: 5.66 us -> none  [body(): lax.psum_scatter((contract_first(flat_w, scaled) + contract_first(flat_x,...]
    unnamed x18 -> x4, local copies, waits for them, and re-layouts: 2 us -> 7.02 us
  transfers between devices with their start and end apart: 3 -> 0, of which waited for: 3 -> 0; matrix products, arithmetic and copies ran while one was open for 3% -> 0% of each run, Pallas kernels for 0% -> 0%
where the time goes in v1:
time: 145 us; the launch traced here: 144 us
  Pallas kernels  134 us (92%)
  local copies, waits for them, and re-layouts  8.21 us (6%)
  between operations  2.42 us (2%)
    pallas_call x1, Pallas kernels, body(): pl.pallas_call(functools.partial(kernel, dims), out_shape=(jax.ShapeDtype...  134 us
    unnamed x4, local copies, waits for them, and re-layouts  7.02 us

profile of v1, /device:TPU:1, one launch (start us, length us, event | category | flops | bytes accessed | tf_op | source)
XLA Modules:
  0.0 144.2 jit_solution(2360743175887032066)
XLA Ops:
  0.6 1.4 copy.11.ids_ref
  2.0 1.4 copy.12.gate_ref
  3.5 133.6 %shard_map.103 = (bf16[1,256,2048]{2,1,0:T(8,128)(2,1)}, f32[128,1024]{1,0:T(8,128)}, f32[8,128]{1,0:T(8,128)}) custom-call(bf16[128,1024]{1,0:T(8,128)(2,1)} %x_ref.1, bf16[128,1024]{1,0:T(8,128)(2,1)} %r_ref.1, bf16[1,1024,2048]{2,1,0:T(8,128)(2,1)} %up_hbm.1, bf16[1,2048,1024]{2,1,0:T(8,128)(2,1)} %down_hbm.1, s32[128,2]{1,0:T(8,128)} %copy.11.ids_ref, ...), custom_call_target="tpu_custom_call" | custom-call | tf_op jit(solution)/shard_map/pallas_call | solution.py:335
  137.0 1.2 slice.3
  138.9 2.3 %copy.15 = bf16[1,256,2048]{2,1,0:T(8,128)(2,1)} copy(bf16[1,256,2048]{2,1,0:T(8,128)(2,1)} %get-tuple-element.12) | data formatting | bytes 2097152
  141.2 1.9 %copy.16 = f32[128,1024]{1,0:T(8,128)} copy(f32[128,1024]{1,0:T(8,128)} %get-tuple-element.13) | data formatting | bytes 1048576

commit v2 on v1

v2 whole, which is shorter than its diff:
```python
import functools

import jax
import jax.numpy as jnp
import numpy as np
from jax import lax
from jax.experimental import pallas as pl
from jax.experimental.pallas import tpu as pltpu
from jax.sharding import PartitionSpec as P

MESH = pl.DeviceIdType.MESH
F32 = jnp.float32
BF16 = jnp.bfloat16
NX, NZ, NC, CAP = 4, 8, 2, 5
TILE = 256


def dot(a, b):
    return lax.dot_general(a, b, (((1,), (0,)), ((), ())), preferred_element_type=F32)


def dot_t(a, b):
    return lax.dot_general(a, b, (((1,), (1,)), ((), ())), preferred_element_type=F32)


def kernel(
    dims,
    x_ref, r_ref, up_hbm, down_hbm, ids_ref, gate_ref, pf_ref, pb_ref,
    grad_ref, ig_ref, pen_ref,
    up, down, sz, rz, sx, rx, ry, act, sg, pc, scaled, xt, wt, gacc,
    sel, selt, small, q_r, q_g, q_y,
    wsem, zs, zr, xs, xr, ys, yr, fs, fr, qs, qr,
):
    nx, nz, nc, ny, cap = dims
    ng = nx * nc
    tok, width = x_ref.shape
    ff = up.shape[1]
    ch = ny
    cw = width // ch
    zrow, grow = ng * cap, nz * cap
    slots = nz * zrow
    e = lax.axis_index("expert")
    y = lax.axis_index("rep")
    x = e // (nz * nc)
    z = (e // nc) % nz
    c = e % nc
    g = x * nc + c

    def z_peer(k):
        zt = lax.rem(z + k, nz)
        return zt, ((x * nz + zt) * nc + c, y)

    def g_peer(k):
        gt = lax.rem(g + k, ng)
        return gt, (((gt // nc) * nz + z) * nc + gt % nc, y)

    def y_peer(k):
        yt = lax.rem(y + k, ny)
        return yt, (e, yt)

    load_up = pltpu.make_async_copy(up_hbm.at[0], up, wsem.at[0])
    load_down = pltpu.make_async_copy(down_hbm.at[0], down, wsem.at[1])

    barrier = pltpu.get_barrier_semaphore()
    peers = (
        [z_peer(k)[1] for k in range(1, nz)]
        + [g_peer(k)[1] for k in range(1, ng)]
        + [y_peer(k)[1] for k in range(1, ny)]
    )
    for peer in peers:
        pl.semaphore_signal(barrier, inc=1, device_id=peer, device_id_type=MESH)
    load_up.start()
    load_down.start()

    zorder = sorted(range(1, nz), key=lambda k: (-min(k, nz - k), k))
    gorder = sorted(range(1, ng), key=lambda k: (-min(k, ng - k), k))

    def z_send(st):
        for k in zorder:
            zt, dev = z_peer(k)
            pltpu.make_async_remote_copy(
                src_ref=sz.at[st, zt], dst_ref=rz.at[st, z],
                send_sem=zs.at[st], recv_sem=zr.at[st],
                device_id=dev, device_id_type=MESH,
            ).start()

    def g_send(st):
        for k in gorder:
            gt, dev = g_peer(k)
            pltpu.make_async_remote_copy(
                src_ref=sx.at[st, gt], dst_ref=rx.at[st, g],
                send_sem=xs.at[st], recv_sem=xr.at[st],
                device_id=dev, device_id_type=MESH,
            ).start()

    def wait_all(ref, st, count, sem):
        part = ref.at[st, pl.ds(0, count)]
        pltpu.make_async_copy(part, part, sem.at[st]).wait()

    def z_wait(st):
        wait_all(rz, st, nz - 1, zr)
        rz[st, z] = sz[st, z]

    def g_wait(st):
        wait_all(rx, st, ng - 1, xr)
        rx[st, g] = sx[st, g]

    def stage(kind, h):
        return "xrow".index(kind) * ch + h

    def ystage(kind, h):
        return "xrw".index(kind) * ch + h

    hg = ng // 2
    halves = (pl.ds(0, hg), pl.ds(hg, ng - hg))

    def y_copy(src, slot, sy, half, d, send, recv):
        _, dev = y_peer(1 if d == 0 else ny - 1)
        return pltpu.make_async_remote_copy(
            src_ref=src.at[halves[half]], dst_ref=ry.at[slot, sy, halves[half]],
            send_sem=send, recv_sem=recv, device_id=dev, device_id_type=MESH,
        )

    def y_home(kind, h, d, half):
        sy = ystage(kind, h)
        return y_copy(
            rx.at[stage(kind, h)], d, sy, half, d, ys.at[d, half, sy], yr.at[d, half, sy]
        )

    def y_hand(kind, h, d):
        sy = ystage(kind, h)
        return y_copy(ry.at[d, sy], 2, sy, d, d, fs.at[d, sy], fr.at[d, sy])

    def y_send(kind, h):
        for i in range(2):
            for d in range(2):
                y_home(kind, h, d, i if d == 0 else 1 - i).start()

    def y_relay(kind, h):
        for d in range(2):
            y_home(kind, h, d, d).wait_recv()
            y_hand(kind, h, d).start()

    def y_wait(kind, b, h):
        if b < 3:
            y_home(kind, h, b - 1, 2 - b).wait_recv()
        else:
            for d in range(2):
                y_hand(kind, h, d).wait_recv()

    def flatten(v):
        return v.astype(F32).reshape(slots, cw).astype(BF16)

    def put(ref, st, v):
        ref[st] = v.reshape(ref.shape[1:]).astype(BF16)

    def chunk(kind, b, h):
        if b == 0:
            return flatten(rx[stage(kind, 0) + h])
        return flatten(ry[b - 1, ystage(kind, 0) + h])

    def cols(h):
        return slice(h * cw, (h + 1) * cw)

    n_exp = nz * ng
    v = ids_ref[...]
    rest = v // nc
    q = (rest % nz) * ng + (rest // nz) * nc + v % nc
    small[0:2, :] = q.astype(F32)
    small[2:4, :] = gate_ref[...]
    small[4:8, :] = jnp.zeros((4, tok), F32)
    small_t = small[...].T
    col_e = lax.broadcasted_iota(jnp.int32, (tok, n_exp), 1).astype(F32)
    onehots = [jnp.where(col_e == small_t[:, k : k + 1], 1.0, 0.0).astype(F32) for k in range(2)]
    count = (onehots[0] + onehots[1]).astype(BF16)
    ti = lax.broadcasted_iota(jnp.int32, (tok, tok), 0)
    tj = lax.broadcasted_iota(jnp.int32, (tok, tok), 1)
    lower = jnp.where(tj < ti, 1.0, 0.0).astype(BF16)
    earlier = dot(lower, count)
    col_s = lax.broadcasted_iota(jnp.int32, (tok, slots), 1).astype(F32)
    for k in range(2):
        slot = jnp.sum(onehots[k] * earlier, axis=1, keepdims=True)
        pos = small_t[:, k : k + 1] * cap + slot
        m = jnp.where(col_s == pos, 1.0, 0.0).astype(F32)
        sel[k] = m.astype(BF16)
        selt[k] = m.T.astype(BF16)

    both = (selt[0].astype(F32) + selt[1].astype(F32)).astype(BF16)
    for h in range(ch):
        put(sz, stage("x", h), dot(both, x_ref[:, cols(h)]))
    pl.semaphore_wait(barrier, len(peers))
    for h in range(ch):
        z_send(stage("x", h))
    for h in range(ch):
        put(sz, stage("r", h), dot(both, r_ref[:, cols(h)]))
        z_send(stage("r", h))

    def forward(kind, h):
        st = stage(kind, h)
        z_wait(st)
        put(sx, st, dot(pf_ref[...], flatten(rz[st])))
        g_send(st)

    def arrive(kind, h):
        g_wait(stage(kind, h))
        y_send(kind, h)

    def gather(kind, b, first=0, last=ch):
        for h in range(first, last):
            act[b, :, cols(h)] = chunk(kind, b, h)

    def tiles(fn):
        @pl.loop(0, ff // TILE)
        def _(i):
            fn(pl.ds(pl.multiple_of(i * TILE, TILE), TILE))

    def pre_task(b):
        gather("x", b)
        xt[b] = chunk("x", b, y).astype(F32).T.astype(BF16)

        def fn(n):
            p = dot(act[b], up[:, n])
            s = 1.0 / (1.0 + jnp.exp(-p))
            sg[b, :, n] = s * (1.0 + p * (1.0 - s))
            pc[b, :, n] = s * (1.0 - s) * (2.0 + p * (1.0 - 2.0 * s))

        tiles(fn)

    def proj_done(b, n, p):
        scaled[b, :, n] = (sg[b, :, n] * p).astype(BF16)
        pc[b, :, n] = p * pc[b, :, n]

    def proj_task(b):
        gather("r", b)
        tiles(lambda n: proj_done(b, n, dot_t(act[b], down[n, :])))

    forward("x", 0)
    forward("x", 1)
    forward("x", 2)
    arrive("x", 0)
    forward("x", 3)
    arrive("x", 1)
    forward("r", 0)
    arrive("x", 2)
    y_relay("x", 0)
    forward("r", 1)
    arrive("x", 3)
    load_up.wait()
    load_down.wait()
    pre_task(0)
    forward("r", 2)
    arrive("r", 0)
    y_relay("x", 1)
    forward("r", 3)
    arrive("r", 1)
    y_relay("x", 2)
    part = (ch // 2) * cw
    gather("r", 0, 0, ch // 2)

    def early_proj(n):
        sg[1, :, n] = dot_t(act[0, :, :part], down[n, :part])

    tiles(early_proj)
    arrive("r", 2)
    arrive("r", 3)
    gather("r", 0, ch // 2, ch)
    tiles(lambda n: proj_done(
        0, n, sg[1, :, n] + dot_t(act[0, :, part:], down[n, part:])
    ))

    for h in range(ch):
        put(sx, stage("o", h), dot_t(scaled[0], up[cols(h), :]))
        g_send(stage("o", h))
    y_relay("x", 3)
    for h in range(ch):
        st = stage("o", h)
        g_wait(st)
        put(sz, st, dot(pb_ref[...], flatten(rx[st])))
        z_send(st)

    g0 = small[...].T[:, 2:3]
    g1 = small[...].T[:, 3:4]

    def combine(h):
        st = stage("o", h)
        z_wait(st)
        got = flatten(rz[st])
        ig = (
            r_ref[:, cols(h)].astype(F32)
            + g0 * dot(sel[0], got)
            + g1 * dot(sel[1], got)
        )
        cot = dot(selt[0], (g0 * ig).astype(BF16)) + dot(selt[1], (g1 * ig).astype(BF16))
        put(sz, stage("w", h), cot)
        z_send(stage("w", h))
        ig_ref[:, cols(h)] = ig
        return jnp.sum(ig * ig, axis=0, keepdims=True)

    y_relay("r", 0)
    for h in range(ch):
        y_wait("x", 1, h)
    pre_task(1)
    squares = combine(0)
    y_relay("r", 1)
    for h in range(ch):
        y_wait("x", 2, h)
    pre_task(2)
    squares = squares + combine(1)
    y_relay("r", 2)
    y_relay("r", 3)
    for h in range(ch):
        y_wait("r", 1, h)
    proj_task(1)
    squares = squares + combine(2)
    for h in range(ch):
        y_wait("r", 2, h)
    proj_task(2)
    squares = squares + combine(3)

    def q_send(buf, me, peer_of, n, st):
        for k in range(1, n):
            _, dev = peer_of(k)
            pltpu.make_async_remote_copy(
                src_ref=buf.at[me], dst_ref=buf.at[me],
                send_sem=qs.at[st], recv_sem=qr.at[st],
                device_id=dev, device_id_type=MESH,
            ).start()

    def q_wait(buf, n, st):
        some = buf.at[pl.ds(0, n - 1)]
        pltpu.make_async_copy(some, some, qr.at[st]).wait()
        pltpu.make_async_copy(some, some, qs.at[st]).wait()
        total = buf[0]
        for i in range(1, n):
            total = total + buf[i]
        return total

    lanes = q_r.shape[2]
    row = squares[:, :lanes]
    for i in range(1, cw // lanes):
        row = row + squares[:, i * lanes : (i + 1) * lanes]
    q_r[z] = jnp.broadcast_to(row * 0.125, q_r.shape[1:])
    q_send(q_r, z, z_peer, nz, 0)

    for h in range(ch):
        y_wait("x", 3, h)
    pre_task(3)
    forward("w", 0)
    for h in range(ch):
        y_wait("r", 3, h)
    proj_task(3)
    forward("w", 1)
    arrive("w", 0)
    q_g[g] = q_wait(q_r, nz, 0)
    q_send(q_g, g, g_peer, ng, 1)
    forward("w", 2)
    arrive("w", 1)
    forward("w", 3)
    arrive("w", 2)
    y_relay("w", 0)
    q_y[y] = q_wait(q_g, ng, 1)
    q_send(q_y, y, y_peer, ny, 2)
    arrive("w", 3)

    most = (ch - 1) * cw

    def early(b):
        gather("w", b, 0, ch - 1)

        def fn(n):
            sg[b, :, n] = dot(act[b, :, :most], up[:most, n])

        tiles(fn)

    def late(b):
        gather("w", b, ch - 1, ch)
        wt[b] = chunk("w", b, y).astype(F32).T.astype(BF16)

        def fn(n):
            s = sg[b, :, n] + dot(act[b, :, most:], up[most:, n])
            pre_grad = (s * pc[b, :, n]).astype(BF16)
            t = dot(wt[b], scaled[b, :, n]) + dot(xt[b], pre_grad)
            if b > 0:
                t = t + gacc[:, n]
            if b < 3:
                gacc[:, n] = t
            else:
                grad_ref[0, :, n] = t.astype(BF16)

        tiles(fn)

    early(0)
    y_relay("w", 1)
    late(0)
    y_relay("w", 2)
    for b in (1, 2):
        for h in range(ch - 1):
            y_wait("w", b, h)
    early(1)
    y_relay("w", 3)
    early(2)
    for b in (1, 2):
        y_wait("w", b, ch - 1)
        late(b)
    for h in range(ch - 1):
        y_wait("w", 3, h)
    early(3)
    y_wait("w", 3, ch - 1)
    late(3)

    total = q_wait(q_y, ny, 2)
    total = jnp.sum(jnp.sum(total, axis=0, keepdims=True), axis=1, keepdims=True)
    pen_ref[...] = jnp.broadcast_to(total, pen_ref.shape)

    for kind in "xrow":
        for h in range(ch):
            st = stage(kind, h)
            wait_all(sz, st, nz - 1, zs)
            wait_all(sx, st, ng - 1, xs)
            if kind != "o":
                for d in range(2):
                    y_home(kind, h, d, 0).wait_send()
                    y_home(kind, h, d, 1).wait_send()
                    y_hand(kind, h, d).wait_send()


def regroup(outer, inner, cap):
    n = outer * inner * cap
    src = np.arange(n).reshape(outer, inner, cap).transpose(1, 0, 2).reshape(-1)
    return jnp.asarray(np.eye(n, dtype=np.float32)[src], BF16)


def body(dims, features, readout, up_weight, down_weight, expert_ids, gate_values):
    nx, nz, nc, ny, cap = dims
    ng = nx * nc
    tok, width = features.shape
    ff = up_weight.shape[2]
    ch = ny
    cw = width // ch
    slots = nz * ng * cap
    lanes = min(cw, 128)
    vm = pl.BlockSpec(memory_space=pltpu.VMEM)
    hbm = pl.BlockSpec(memory_space=pl.ANY)
    dma = pltpu.SemaphoreType.DMA
    zbuf = pltpu.VMEM((4 * ch, nz, ng * cap, cw), BF16)
    gbuf = pltpu.VMEM((4 * ch, ng, nz * cap, cw), BF16)
    grad, ig, pen = pl.pallas_call(
        functools.partial(kernel, dims),
        out_shape=(
            jax.ShapeDtypeStruct((1, width // ny, ff), BF16),
            jax.ShapeDtypeStruct((tok, width), F32),
            jax.ShapeDtypeStruct((8, 128), F32),
        ),
        in_specs=[vm, vm, hbm, hbm, vm, vm, vm, vm],
        out_specs=(vm, vm, vm),
        scratch_shapes=[
            pltpu.VMEM((width, ff), BF16),
            pltpu.VMEM((ff, width), BF16),
            zbuf, zbuf, gbuf, gbuf,
            pltpu.VMEM((3, 3 * ch, ng, nz * cap, cw), BF16),
            pltpu.VMEM((4, slots, width), BF16),
            pltpu.VMEM((4, slots, ff), F32),
            pltpu.VMEM((4, slots, ff), F32),
            pltpu.VMEM((4, slots, ff), BF16),
            pltpu.VMEM((4, cw, slots), BF16),
            pltpu.VMEM((4, cw, slots), BF16),
            pltpu.VMEM((cw, ff), F32),
            pltpu.VMEM((2, tok, slots), BF16),
            pltpu.VMEM((2, slots, tok), BF16),
            pltpu.VMEM((8, tok), F32),
            pltpu.VMEM((nz, 8, lanes), F32),
            pltpu.VMEM((ng, 8, lanes), F32),
            pltpu.VMEM((ny, 8, lanes), F32),
            dma((2,)), dma((4 * ch,)), dma((4 * ch,)), dma((4 * ch,)), dma((4 * ch,)),
            dma((2, 2, 3 * ch)), dma((2, 2, 3 * ch)),
            dma((2, 3 * ch)), dma((2, 3 * ch)),
            dma((3,)), dma((3,)),
        ],
        compiler_params=pltpu.CompilerParams(
            collective_id=0, has_side_effects=True, vmem_limit_bytes=67043328
        ),
    )(
        features, readout, up_weight, down_weight, expert_ids.T, gate_values.T,
        regroup(nz, ng, cap), regroup(ng, nz, cap),
    )
    groups = nz * ng
    penalty = pen[0, 0] / (2.0 * tok * groups * ny * width)
    return grad, ig, penalty


def solution(mesh, dims=None):
    if dims is None:
        dims = (NX, NZ, NC, mesh.shape["rep"], CAP)
    both = ("expert", "rep")
    return jax.shard_map(
        functools.partial(body, dims),
        mesh=mesh,
        in_specs=(
            P(both, None), P(both, None),
            P("expert", None, None), P("expert", None, None),
            P(both, None), P(both, None),
        ),
        out_specs=(P("expert", "rep", None), P(both, None), P()),
        check_vma=False,
    )
```

time: 145 us -> 131 us (0.903)
  Pallas kernels: 134 us -> 123 us
  local copies, waits for them, and re-layouts: 8.21 us -> 5.39 us
    pallas_call x1, Pallas kernels: 134 us -> 123 us  [body(): pl.pallas_call(functools.partial(kernel, dims), out_shape=(jax.ShapeDtype...]
    unnamed x4 -> x2, local copies, waits for them, and re-layouts: 7.02 us -> 4.19 us
where the time goes in v2:
time: 131 us
  Pallas kernels  123 us (94%)
  local copies, waits for them, and re-layouts  5.39 us (4%)
  between operations  2.42 us (2%)
    pallas_call x1, Pallas kernels, body(): pl.pallas_call(functools.partial(kernel, dims), out_shape=(jax.ShapeDtype...  123 us
    unnamed x2, local copies, waits for them, and re-layouts  4.19 us

profile of v2, /device:TPU:1, one launch (start us, length us, event | category | flops | bytes accessed | tf_op | source)
XLA Modules:
  0.0 130.9 jit_solution(2715319582274174867)
XLA Ops:
  0.6 123.1 %shard_map.103 = (bf16[1,256,2048]{2,1,0:T(8,128)(2,1)}, f32[128,1024]{1,0:T(8,128)}, f32[8,128]{1,0:T(8,128)}) custom-call(bf16[128,1024]{1,0:T(8,128)(2,1)} %x_ref.1, bf16[128,1024]{1,0:T(8,128)(2,1)} %r_ref.1, bf16[1,1024,2048]{2,1,0:T(8,128)(2,1)} %up_hbm.1, bf16[1,2048,1024]{2,1,0:T(8,128)(2,1)} %down_hbm.1, s32[2,128]{1,0:T(2,128)} %bitcast.3, ...), custom_call_target="tpu_custom_call" | custom-call | tf_op jit(solution)/shard_map/pallas_call | solution.py:447
  123.7 1.2 slice.3
  125.5 2.3 %copy.13 = bf16[1,256,2048]{2,1,0:T(8,128)(2,1)} copy(bf16[1,256,2048]{2,1,0:T(8,128)(2,1)} %get-tuple-element.12) | data formatting | bytes 2097152
  127.9 1.9 %copy.14 = f32[128,1024]{1,0:T(8,128)} copy(f32[128,1024]{1,0:T(8,128)} %get-tuple-element.13) | data formatting | bytes 1048576

commit v3 on v2

--- a/solution.py
+++ b/solution.py
@@ -12,7 +12,7 @@
 F32 = jnp.float32
 BF16 = jnp.bfloat16
 NX, NZ, NC, CAP = 4, 8, 2, 5
-TILE = 256
+TILE = 512
 
 
 def dot(a, b):
@@ -25,11 +25,12 @@
 
 def kernel(
     dims,
-    x_ref, r_ref, up_hbm, down_hbm, ids_ref, gate_ref, pf_ref, pb_ref,
-    grad_ref, ig_ref, pen_ref,
+    x_hbm, r_hbm, up_hbm, down_hbm, ids_hbm, gate_hbm, pf_hbm, pb_hbm,
+    grad_hbm, ig_hbm, pen_hbm,
+    x_ref, r_ref, ids_ref, gate_ref, pf_ref, pb_ref, grad_ref, ig_ref, pen_ref,
     up, down, sz, rz, sx, rx, ry, act, sg, pc, scaled, xt, wt, gacc,
     sel, selt, small, q_r, q_g, q_y,
-    wsem, zs, zr, xs, xr, ys, yr, fs, fr, qs, qr,
+    wsem, osem, zs, zr, xs, xr, ys, yr, fs, fr, qs, qr,
 ):
     nx, nz, nc, ny, cap = dims
     ng = nx * nc
@@ -58,9 +59,6 @@
         yt = lax.rem(y + k, ny)
         return yt, (e, yt)
 
-    load_up = pltpu.make_async_copy(up_hbm.at[0], up, wsem.at[0])
-    load_down = pltpu.make_async_copy(down_hbm.at[0], down, wsem.at[1])
-
     barrier = pltpu.get_barrier_semaphore()
     peers = (
         [z_peer(k)[1] for k in range(1, nz)]
@@ -69,8 +67,13 @@
     )
     for peer in peers:
         pl.semaphore_signal(barrier, inc=1, device_id=peer, device_id_type=MESH)
-    load_up.start()
-    load_down.start()
+    pairs = (
+        (ids_hbm, ids_ref), (gate_hbm, gate_ref), (x_hbm, x_ref), (r_hbm, r_ref),
+        (pf_hbm, pf_ref), (pb_hbm, pb_ref), (up_hbm.at[0], up), (down_hbm.at[0], down),
+    )
+    loads = [pltpu.make_async_copy(a, b, wsem.at[i]) for i, (a, b) in enumerate(pairs)]
+    for load in loads:
+        load.start()
 
     zorder = sorted(range(1, nz), key=lambda k: (-min(k, nz - k), k))
     gorder = sorted(range(1, ng), key=lambda k: (-min(k, ng - k), k))
@@ -163,6 +166,8 @@
         return slice(h * cw, (h + 1) * cw)
 
     n_exp = nz * ng
+    loads[0].wait()
+    loads[1].wait()
     v = ids_ref[...]
     rest = v // nc
     q = (rest % nz) * ng + (rest // nz) * nc + v % nc
@@ -186,11 +191,13 @@
         selt[k] = m.T.astype(BF16)
 
     both = (selt[0].astype(F32) + selt[1].astype(F32)).astype(BF16)
+    loads[2].wait()
     for h in range(ch):
         put(sz, stage("x", h), dot(both, x_ref[:, cols(h)]))
     pl.semaphore_wait(barrier, len(peers))
     for h in range(ch):
         z_send(stage("x", h))
+    loads[3].wait()
     for h in range(ch):
         put(sz, stage("r", h), dot(both, r_ref[:, cols(h)]))
         z_send(stage("r", h))
@@ -234,6 +241,8 @@
         gather("r", b)
         tiles(lambda n: proj_done(b, n, dot_t(act[b], down[n, :])))
 
+    loads[4].wait()
+    loads[5].wait()
     forward("x", 0)
     forward("x", 1)
     forward("x", 2)
@@ -245,8 +254,8 @@
     y_relay("x", 0)
     forward("r", 1)
     arrive("x", 3)
-    load_up.wait()
-    load_down.wait()
+    loads[6].wait()
+    loads[7].wait()
     pre_task(0)
     forward("r", 2)
     arrive("r", 0)
@@ -271,12 +280,16 @@
     for h in range(ch):
         put(sx, stage("o", h), dot_t(scaled[0], up[cols(h), :]))
         g_send(stage("o", h))
-    y_relay("x", 3)
-    for h in range(ch):
+
+    def back(h):
         st = stage("o", h)
         g_wait(st)
         put(sz, st, dot(pb_ref[...], flatten(rx[st])))
-        z_send(st)
+
+    back(0)
+    z_send(stage("o", 0))
+    back(1)
+    z_send(stage("o", 1))
 
     g0 = small[...].T[:, 2:3]
     g1 = small[...].T[:, 3:4]
@@ -296,26 +309,37 @@
         ig_ref[:, cols(h)] = ig
         return jnp.sum(ig * ig, axis=0, keepdims=True)
 
+    def y_all(kind, b):
+        for h in range(ch):
+            y_wait(kind, b, h)
+
+    y_relay("x", 3)
     y_relay("r", 0)
-    for h in range(ch):
-        y_wait("x", 1, h)
+    y_all("x", 1)
     pre_task(1)
+    back(2)
+    back(3)
     squares = combine(0)
+    z_send(stage("o", 2))
     y_relay("r", 1)
-    for h in range(ch):
-        y_wait("x", 2, h)
+    y_all("x", 2)
     pre_task(2)
     squares = squares + combine(1)
+    z_send(stage("o", 3))
     y_relay("r", 2)
+    forward("w", 0)
     y_relay("r", 3)
-    for h in range(ch):
-        y_wait("r", 1, h)
+    y_all("r", 1)
     proj_task(1)
     squares = squares + combine(2)
-    for h in range(ch):
-        y_wait("r", 2, h)
+    arrive("w", 0)
+    y_all("r", 2)
     proj_task(2)
+    forward("w", 1)
     squares = squares + combine(3)
+    save_ig = pltpu.make_async_copy(ig_ref, ig_hbm, osem.at[1])
+    save_ig.start()
+    arrive("w", 1)
 
     def q_send(buf, me, peer_of, n, st):
         for k in range(1, n):
@@ -342,25 +366,17 @@
     q_r[z] = jnp.broadcast_to(row * 0.125, q_r.shape[1:])
     q_send(q_r, z, z_peer, nz, 0)
 
-    for h in range(ch):
-        y_wait("x", 3, h)
+    y_all("x", 3)
     pre_task(3)
-    forward("w", 0)
-    for h in range(ch):
-        y_wait("r", 3, h)
-    proj_task(3)
-    forward("w", 1)
-    arrive("w", 0)
+    y_relay("w", 0)
+    forward("w", 2)
     q_g[g] = q_wait(q_r, nz, 0)
     q_send(q_g, g, g_peer, ng, 1)
-    forward("w", 2)
-    arrive("w", 1)
+    y_all("r", 3)
+    proj_task(3)
     forward("w", 3)
     arrive("w", 2)
-    y_relay("w", 0)
-    q_y[y] = q_wait(q_g, ng, 1)
-    q_send(q_y, y, y_peer, ny, 2)
-    arrive("w", 3)
+    y_relay("w", 1)
 
     most = (ch - 1) * cw
 
@@ -386,31 +402,37 @@
                 gacc[:, n] = t
             else:
                 grad_ref[0, :, n] = t.astype(BF16)
+                pltpu.make_async_copy(
+                    grad_ref.at[:, :, n], grad_hbm.at[:, :, n], osem.at[0]
+                ).start()
 
         tiles(fn)
 
     early(0)
-    y_relay("w", 1)
+    q_y[y] = q_wait(q_g, ng, 1)
+    q_send(q_y, y, y_peer, ny, 2)
+    arrive("w", 3)
+    y_relay("w", 2)
     late(0)
-    y_relay("w", 2)
     for b in (1, 2):
         for h in range(ch - 1):
             y_wait("w", b, h)
-    early(1)
-    y_relay("w", 3)
-    early(2)
+        early(b)
+        if b == 1:
+            y_relay("w", 3)
     for b in (1, 2):
         y_wait("w", b, ch - 1)
         late(b)
     for h in range(ch - 1):
         y_wait("w", 3, h)
     early(3)
-    y_wait("w", 3, ch - 1)
-    late(3)
-
     total = q_wait(q_y, ny, 2)
     total = jnp.sum(jnp.sum(total, axis=0, keepdims=True), axis=1, keepdims=True)
     pen_ref[...] = jnp.broadcast_to(total, pen_ref.shape)
+    save_pen = pltpu.make_async_copy(pen_ref, pen_hbm, osem.at[2])
+    save_pen.start()
+    y_wait("w", 3, ch - 1)
+    late(3)
 
     for kind in "xrow":
         for h in range(ch):
@@ -422,6 +444,34 @@
                     y_home(kind, h, d, 0).wait_send()
                     y_home(kind, h, d, 1).wait_send()
                     y_hand(kind, h, d).wait_send()
+    pltpu.make_async_copy(grad_ref, grad_hbm, osem.at[0]).wait()
+    save_ig.wait()
+    save_pen.wait()
+
+
+def finish(scale, grad_in, ig_in, pen_in, grad_out, ig_out, pen_out, gbuf, ibuf, isem, osem):
+    steps = []
+    parts = 2
+    for i in range(parts):
+        n = grad_in.shape[1] // parts
+        steps.append((grad_in, gbuf, grad_out, (slice(None), pl.ds(i * n, n))))
+    steps.append((ig_in, ibuf, ig_out, (slice(None),)))
+    reads = [
+        pltpu.make_async_copy(a.at[at], v.at[at], isem.at[i])
+        for i, (a, v, b, at) in enumerate(steps)
+    ]
+    writes = [
+        pltpu.make_async_copy(v.at[at], b.at[at], osem.at[i])
+        for i, (a, v, b, at) in enumerate(steps)
+    ]
+    for read in reads:
+        read.start()
+    pen_out[...] = pen_in[0:1, 0:1] * scale
+    for read, write in zip(reads, writes):
+        read.wait()
+        write.start()
+    for write in writes:
+        write.wait()
 
 
 def regroup(outer, inner, cap):
@@ -451,9 +501,18 @@
             jax.ShapeDtypeStruct((tok, width), F32),
             jax.ShapeDtypeStruct((8, 128), F32),
         ),
-        in_specs=[vm, vm, hbm, hbm, vm, vm, vm, vm],
-        out_specs=(vm, vm, vm),
+        in_specs=[hbm] * 8,
+        out_specs=(hbm, hbm, hbm),
         scratch_shapes=[
+            pltpu.VMEM((tok, width), BF16),
+            pltpu.VMEM((tok, width), BF16),
+            pltpu.VMEM((2, tok), jnp.int32),
+            pltpu.VMEM((2, tok), F32),
+            pltpu.VMEM((slots, slots), BF16),
+            pltpu.VMEM((slots, slots), BF16),
+            pltpu.VMEM((1, width // ny, ff), BF16),
+            pltpu.VMEM((tok, width), F32),
+            pltpu.VMEM((8, 128), F32),
             pltpu.VMEM((width, ff), BF16),
             pltpu.VMEM((ff, width), BF16),
             zbuf, zbuf, gbuf, gbuf,
@@ -471,7 +530,7 @@
             pltpu.VMEM((nz, 8, lanes), F32),
             pltpu.VMEM((ng, 8, lanes), F32),
             pltpu.VMEM((ny, 8, lanes), F32),
-            dma((2,)), dma((4 * ch,)), dma((4 * ch,)), dma((4 * ch,)), dma((4 * ch,)),
+            dma((8,)), dma((3,)), dma((4 * ch,)), dma((4 * ch,)), dma((4 * ch,)), dma((4 * ch,)),
             dma((2, 2, 3 * ch)), dma((2, 2, 3 * ch)),
             dma((2, 3 * ch)), dma((2, 3 * ch)),
             dma((3,)), dma((3,)),
@@ -483,9 +542,22 @@
         features, readout, up_weight, down_weight, expert_ids.T, gate_values.T,
         regroup(nz, ng, cap), regroup(ng, nz, cap),
     )
-    groups = nz * ng
-    penalty = pen[0, 0] / (2.0 * tok * groups * ny * width)
-    return grad, ig, penalty
+    scale = 1.0 / (2.0 * tok * nz * ng * ny * width)
+    grad, ig, pen = pl.pallas_call(
+        functools.partial(finish, scale),
+        out_shape=(
+            jax.ShapeDtypeStruct(grad.shape, BF16),
+            jax.ShapeDtypeStruct(ig.shape, F32),
+            jax.ShapeDtypeStruct((1, 1), F32),
+        ),
+        in_specs=[hbm, hbm, vm],
+        out_specs=(hbm, hbm, vm),
+        scratch_shapes=[
+            pltpu.VMEM(grad.shape, BF16), pltpu.VMEM(ig.shape, F32), dma((3,)), dma((3,)),
+        ],
+        compiler_params=pltpu.CompilerParams(vmem_limit_bytes=67043328),
+    )(grad, ig, pen)
+    return grad, ig, pen.reshape(())
 
 
 def solution(mesh, dims=None):

time: 131 us -> 115 us (0.88)
  Pallas kernels: 123 us -> 113 us
  local copies, waits for them, and re-layouts: 5.39 us -> 0 us
  between operations: 2.42 us -> 0.8 us
    pallas_call x1, Pallas kernels: 123 us -> 110 us  [body(): pl.pallas_call(functools.partial(kernel, dims), out_shape=(jax.ShapeDtype...]
    unnamed x2 -> x0, local copies, waits for them, and re-layouts: 4.19 us -> none
    pallas_call x0 -> x1, Pallas kernels: none -> 3.41 us  [body(): pl.pallas_call(functools.partial(finish, scale), out_shape=(jax.ShapeDtyp...]
where the time goes in v3:
time: 115 us; the launch traced here: 114 us
  Pallas kernels  113 us (98%)
    pallas_call x1, Pallas kernels, body(): pl.pallas_call(functools.partial(kernel, dims), out_shape=(jax.ShapeDtype...  110 us
    pallas_call x1, Pallas kernels, body(): pl.pallas_call(functools.partial(finish, scale), out_shape=(jax.ShapeDtyp...  3.41 us

profile of v3, /device:TPU:1, one launch (start us, length us, event | category | flops | bytes accessed | tf_op | source)
XLA Modules:
  0.0 114.1 jit_solution(11945040944193688720)
XLA Ops:
  0.6 109.9 %shard_map.103 = (bf16[1,256,2048]{2,1,0:T(8,128)(2,1)}, f32[128,1024]{1,0:T(8,128)}, f32[8,128]{1,0:T(8,128)}) custom-call(bf16[128,1024]{1,0:T(8,128)(2,1)} %x_hbm.1, bf16[128,1024]{1,0:T(8,128)(2,1)} %r_hbm.1, bf16[1,1024,2048]{2,1,0:T(8,128)(2,1)} %up_hbm.1, bf16[1,2048,1024]{2,1,0:T(8,128)(2,1)} %down_hbm.1, s32[2,128]{1,0:T(2,128)} %bitcast.3, ...), custom_call_target="tpu_custom_call" | custom-call | tf_op jit(solution)/shard_map/pallas_call | solution.py:497
  110.5 3.4 %shard_map.104 = (bf16[1,256,2048]{2,1,0:T(8,128)(2,1)}, f32[128,1024]{1,0:T(8,128)}, f32[1,1]{1,0:T(1,128)}) custom-call(bf16[1,256,2048]{2,1,0:T(8,128)(2,1)} %get-tuple-element.9.grad_in, f32[128,1024]{1,0:T(8,128)} %get-tuple-element.10.ig_in, f32[8,128]{1,0:T(8,128)} %get-tuple-element.11.pen_in), custom_call_target="tpu_custom_call" | custom-call | tf_op jit(solution)/shard_map/pallas_call | solution.py:546

commit v4 on v3

--- a/solution.py
+++ b/solution.py
@@ -12,7 +12,7 @@
 F32 = jnp.float32
 BF16 = jnp.bfloat16
 NX, NZ, NC, CAP = 4, 8, 2, 5
-TILE = 512
+TILE = 1024
 
 
 def dot(a, b):
@@ -263,16 +263,16 @@
     forward("r", 3)
     arrive("r", 1)
     y_relay("x", 2)
-    part = (ch // 2) * cw
-    gather("r", 0, 0, ch // 2)
+    part = (ch - 1) * cw
+    arrive("r", 2)
+    gather("r", 0, 0, ch - 1)
 
     def early_proj(n):
         sg[1, :, n] = dot_t(act[0, :, :part], down[n, :part])
 
     tiles(early_proj)
-    arrive("r", 2)
     arrive("r", 3)
-    gather("r", 0, ch // 2, ch)
+    gather("r", 0, ch - 1, ch)
     tiles(lambda n: proj_done(
         0, n, sg[1, :, n] + dot_t(act[0, :, part:], down[n, part:])
     ))

time: 115 us -> 112 us (0.974)
  Pallas kernels: 113 us -> 110 us
    pallas_call x1, Pallas kernels: 110 us -> 107 us  [body(): pl.pallas_call(functools.partial(kernel, dims), out_shape=(jax.ShapeDtype...]
where the time goes in v4:
time: 112 us; the launch traced here: 111 us
  Pallas kernels  110 us (98%)
    pallas_call x1, Pallas kernels, body(): pl.pallas_call(functools.partial(kernel, dims), out_shape=(jax.ShapeDtype...  107 us
    pallas_call x1, Pallas kernels, body(): pl.pallas_call(functools.partial(finish, scale), out_shape=(jax.ShapeDtyp...  3.41 us

profile of v4, /device:TPU:1, one launch (start us, length us, event | category | flops | bytes accessed | tf_op | source)
XLA Modules:
  0.0 111.0 jit_solution(18064271607317569640)
XLA Ops:
  0.6 106.8 %shard_map.103 = (bf16[1,256,2048]{2,1,0:T(8,128)(2,1)}, f32[128,1024]{1,0:T(8,128)}, f32[8,128]{1,0:T(8,128)}) custom-call(bf16[128,1024]{1,0:T(8,128)(2,1)} %x_hbm.1, bf16[128,1024]{1,0:T(8,128)(2,1)} %r_hbm.1, bf16[1,1024,2048]{2,1,0:T(8,128)(2,1)} %up_hbm.1, bf16[1,2048,1024]{2,1,0:T(8,128)(2,1)} %down_hbm.1, s32[2,128]{1,0:T(2,128)} %bitcast.3, ...), custom_call_target="tpu_custom_call" | custom-call | tf_op jit(solution)/shard_map/pallas_call | solution.py:497
  107.4 3.4 %shard_map.104 = (bf16[1,256,2048]{2,1,0:T(8,128)(2,1)}, f32[128,1024]{1,0:T(8,128)}, f32[1,1]{1,0:T(1,128)}) custom-call(bf16[1,256,2048]{2,1,0:T(8,128)(2,1)} %get-tuple-element.9.grad_in, f32[128,1024]{1,0:T(8,128)} %get-tuple-element.10.ig_in, f32[8,128]{1,0:T(8,128)} %get-tuple-element.11.pen_in), custom_call_target="tpu_custom_call" | custom-call | tf_op jit(solution)/shard_map/pallas_call | solution.py:546
